TPU v7x, 32 devices: a whole 2x2x4 slice. The times are simulated.
32 devices in a mesh: dp: 2 (over core), row: 2 (over x), col: 8 (over z, y).
Axes of the slice: x: 2, y: 2, z: 4, core: 2. Of those that a mesh axis runs over, the one named last changes fastest.
Arguments:
- hidden: bfloat16 [512, 28672], P(('dp', 'row'), 'col'), may hold values from -0.25 to 0.25
- upstream: bfloat16 [512, 8192], P('col', ('dp', 'row')), may hold values from -6 to 6
- weight: bfloat16 [28672, 8192], P('col', ('dp', 'row')), may hold values from -0.03125 to 0.03125
Outputs:
- input_grad: bfloat16 [512, 28672], P(('dp', 'row'), 'col')
- weight_grad: float32 [28672, 8192], P('col', ('dp', 'row'))
All inputs are finite; a program needn't handle non-finite values.
Results may differ from a plain program's by a relative error of at most 0.014.
Values may be sent and summed in bfloat16 or wider, within the bound.
No kernel may reach another device: no remote copies, remote signals or barrier semaphores. Data moves between devices by JAX's collectives and lax.ppermute only.
A program may use at most 128 MiB of HBM per device.

v0:
```python
import jax
import jax.numpy as jnp
from jax import lax
from jax.sharding import PartitionSpec as P


def local(hidden, upstream, weight):
    gathered = lax.all_gather(upstream, "col", axis=0, tiled=True)
    picked = gathered
    weight_grad = lax.dot_general(
        lax.all_gather(hidden, ("dp", "row"), axis=0, tiled=True),
        picked,
        (((0,), (0,)), ((), ())),
        preferred_element_type=jnp.float32,
    )
    picked = gathered
    summed = lax.psum_scatter(
        lax.dot_general(
            picked, weight, (((1,), (1,)), ((), ())), preferred_element_type=jnp.float32
        ).astype(jnp.bfloat16),
        ("dp", "row"),
        scatter_dimension=0,
        tiled=True,
    )
    return (summed, weight_grad)


def solution(mesh):
    return jax.shard_map(
        local,
        mesh=mesh,
        in_specs=(P(("dp", "row"), "col"), P("col", ("dp", "row")), P("col", ("dp", "row"))),
        out_specs=(P(("dp", "row"), "col"), P("col", ("dp", "row"))),
        check_vma=False,
    )
```

profile of v0, /device:TPU:0, one launch (start us, length us, event | category | flops | bytes accessed | tf_op | source)
XLA Modules:
  0.0 144.4 jit_solution(2953297876974728090)
XLA Ops:
  7.2 0.0 all-gather.3.cloned.1.call-start
  7.2 0.7 all-gather.3.cloned.1.call-update
  7.9 0.0 all-gather.5.cloned.1.call-start
  7.9 0.7 all-gather.5.cloned.1.call-update
  8.6 0.0 reduce-scatter.2.cloned.1.call-start
  8.7 53.2 %all-gather.3.cloned.1.call-done = bf16[512,2048]{1,0:T(8,128)(2,1)} async-done(((bf16[64,2048]{1,0:T(8,128)(2,1)}), bf16[512,2048]{1,0:T(8,128)(2,1)}) %all-gather.3.cloned.1.call-update) | async-done | bytes 2097168 | tf_op jit(solution)/shard_map/all_gather | solution.py:8
  61.9 13.0 %convolution_convert_fusion = bf16[512,3584]{1,0:T(8,128)(2,1)} fusion(bf16[512,2048]{1,0:T(8,128)(2,1)} %all-gather.3.cloned.1.call-done, bf16[3584,2048]{1,0:T(8,128)(2,1)} %param.5), kind=kOutput, calls=%fused_computation | convolution fusion | flops 7518027776 | bytes 20447232 | tf_op jit(solution)/shard_map/dot_general | solution.py:18
  74.9 0.0 copy-start
  74.9 0.0 reduce-scatter.2.cloned.1.call-update
  74.9 18.6 %all-gather.5.cloned.1.call-done = bf16[512,3584]{1,0:T(8,128)(2,1)} async-done(((bf16[128,3584]{1,0:T(8,128)(2,1)}), bf16[512,3584]{1,0:T(8,128)(2,1)}) %all-gather.5.cloned.1.call-update) | async-done | bytes 3670032 | tf_op jit(solution)/shard_map/all_gather | solution.py:11
  93.5 0.0 copy-done
  93.5 17.2 %fusion = f32[3584,2048]{1,0:T(8,128)} fusion(bf16[512,3584]{1,0:T(8,128)(2,1)} %all-gather.5.cloned.1.call-done, bf16[512,2048]{1,0:T(8,128)(2,1)S(1)} %copy-done), kind=kOutput, calls=%fused_computation.1 | convolution fusion | flops 7516192768 | bytes 35127296 | tf_op jit(solution)/shard_map/dot_general | solution.py:10
  110.7 27.2 %reduce-scatter.2.cloned.1.call-done = bf16[128,3584]{1,0:T(8,128)(2,1)} async-done(((bf16[512,3584]{1,0:T(8,128)(2,1)}), bf16[128,3584]{1,0:T(8,128)(2,1)}) %reduce-scatter.2.cloned.1.call-update) | async-done | bytes 917520 | tf_op jit(solution)/shard_map/reduce_scatter | solution.py:17
Async XLA Ops:
  7.2 54.8 %all-gather.3.cloned.1.call-start = ((), (), s32[]{:S(2)}) async-start(), calls=%async_computation.1 | async-start | bytes 2359296 | tf_op jit(solution)/shard_map/all_gather | solution.py:8
  7.9 85.6 %all-gather.5.cloned.1.call-start = ((), (), s32[]{:S(2)}) async-start(), calls=%async_computation.3 | async-start | bytes 4587520 | tf_op jit(solution)/shard_map/all_gather | solution.py:11
  8.6 129.3 %reduce-scatter.2.cloned.1.call-start = ((), (), s32[]{:S(2)}) async-start(), calls=%async_computation.2 | async-start | bytes 4587520 | tf_op jit(solution)/shard_map/reduce_scatter | solution.py:17
  74.9 18.6 %copy-start = (bf16[512,2048]{1,0:T(8,128)(2,1)S(1)}, bf16[512,2048]{1,0:T(8,128)(2,1)}, u32[]{:S(2)}) copy-start(bf16[512,2048]{1,0:T(8,128)(2,1)} %all-gather.3.cloned.1.call-done) | copy-start | bytes 6291460
Sparse Core Ops, SparseCore 0:
  10.1 51.7 all-gather.2
  63.5 29.9 all-gather.4
  96.7 41.2 reduce-scatter.1
where the time goes:
time: 145 us; the launch traced here: 144 us
  waiting for transfers between devices  100 us (69%)
  matrix products  30.1 us (21%)
  between operations  13.7 us (9%)
    all_gather x1, waiting for transfers between devices, local(): gathered = lax.all_gather(upstream, 'col', axis=0, tiled=True)  53.2 us
    reduce_scatter x1, waiting for transfers between devices, local(): lax.psum_scatter(lax.dot_general(picked, weight, (((1,), (1,)), ((), ()))...  27.2 us
    all_gather x1, waiting for transfers between devices, local(): lax.all_gather(hidden, ('dp', 'row'), axis=0, tiled=True)  18.6 us
    dot_general x1, matrix products, local(): lax.dot_general(lax.all_gather(hidden, ('dp', 'row'), axis=0, tiled=True)...  17.2 us
    dot_general x1, matrix products, local(): lax.dot_general(picked, weight, (((1,), (1,)), ((), ())), preferred_eleme...  13 us
  transfers between devices with their start and end apart: 3, of which 3 were waited for; matrix products, arithmetic and copies ran while one was open for 21% of the time, Pallas kernels for 0%

commit v1 on v0

v1 whole, which is shorter than its diff:
```python
import jax
import jax.numpy as jnp
from jax import lax
from jax.experimental import pallas as pl
from jax.experimental.pallas import tpu as pltpu
from jax.sharding import PartitionSpec as P


SHARES = (0, 0.3, 0.75, 1)
RING = 4
GRANT_T = 12
GRANT_W = 20
GRANT_S = 6
FETCHES = 4
TOKENS = ("dp", "row")
ALL = ("dp", "row", "col")


def divisor(n, most):
    fits = [b for b in range(128, most + 1, 128) if n % b == 0]
    return fits[-1] if fits else n


def plain(hidden, upstream, weight):
    gathered = lax.all_gather(upstream, "col", axis=0, tiled=True)
    weight_grad = lax.dot_general(
        lax.all_gather(hidden, TOKENS, axis=0, tiled=True),
        gathered,
        (((0,), (0,)), ((), ())),
        preferred_element_type=jnp.float32,
    )
    summed = lax.psum_scatter(
        lax.dot_general(
            gathered, weight, (((1,), (1,)), ((), ())), preferred_element_type=jnp.float32
        ).astype(jnp.bfloat16),
        TOKENS,
        scatter_dimension=0,
        tiled=True,
    )
    return summed, weight_grad


VMEM = pl.BlockSpec(memory_space=pltpu.VMEM)
HBM = pl.BlockSpec(memory_space=pltpu.HBM)


def halves(pieces, ups, t):
    kept = lax.rem(lax.axis_index("col"), 2) == lax.axis_index("dp")
    n = len(pieces) // 2
    first = jnp.where(kept, 0, n * t)
    for i in range(n):
        ups[pl.ds(pl.multiple_of(first + i * t, t), t), :] = pieces[2 * i][...]
        ups[pl.ds(pl.multiple_of(n * t - first + i * t, t), t), :] = pieces[2 * i + 1][...]


def fetched(weight, part):
    ff, d = weight.shape
    half = ff // 2
    cb = half // FETCHES

    def body(w, held, sems):
        def fetch(i):
            return pltpu.make_async_copy(w.at[pl.ds(part * half + i * cb, cb), :], held.at[pl.ds(i * cb, cb), :], sems.at[i])

        for i in range(FETCHES):
            fetch(i).start()
        for i in range(FETCHES):
            fetch(i).wait()

    return pl.pallas_call(
        body,
        in_specs=[HBM],
        out_specs=VMEM,
        out_shape=jax.ShapeDtypeStruct((half, d), weight.dtype),
        scratch_shapes=[pltpu.SemaphoreType.DMA((FETCHES,))],
        compiler_params=pltpu.CompilerParams(vmem_limit_bytes=GRANT_S << 20),
        cost_estimate=pl.CostEstimate(flops=d * half, bytes_accessed=2 * d * half, transcendentals=0),
    )(pltpu.with_memory_space_constraint(weight, pltpu.HBM))


def block_terms(slots, weights):
    t, d = slots[0][0].shape
    half = weights[0].shape[0]
    n = len(slots)
    cb = divisor(half, 896)
    steps = half // cb

    def body(*refs):
        u, w = refs[: 2 * n], refs[2 * n : 2 * n + 2]
        keep, give, ups = refs[2 * n + 2 :]
        halves(u, ups, t)
        for h in range(2):

            def step(i, carry):
                term = lax.dot_general(
                    ups[...],
                    w[h][pl.ds(pl.multiple_of(i * cb, cb), cb), :],
                    (((1,), (1,)), ((), ())),
                    preferred_element_type=jnp.float32,
                ).astype(jnp.bfloat16)
                here = pl.ds(pl.multiple_of(h * half + i * cb, cb), cb)
                keep[:, here] = term[: n * t]
                give[:, here] = term[n * t :]
                return carry

            lax.fori_loop(0, steps, step, 0)

    out = jax.ShapeDtypeStruct((n * t, 2 * half), jnp.bfloat16)
    return pl.pallas_call(
        body,
        in_specs=[VMEM] * (2 * n + 2),
        out_specs=[VMEM] * 2,
        out_shape=[out, out],
        scratch_shapes=[pltpu.VMEM((2 * n * t, d), jnp.bfloat16)],
        compiler_params=pltpu.CompilerParams(vmem_limit_bytes=GRANT_T << 20),
        cost_estimate=pl.CostEstimate(flops=8 * n * t * d * half, bytes_accessed=4 * d * half, transcendentals=0),
    )(*[x for pair in slots for x in pair], *weights)


def weight_gradient(pieces, ups, rows, part, into):
    first = part == 0
    slots = ups if first else []
    t, d = slots[0][0].shape if first else (ups.shape[0] // 8, ups.shape[1])
    m, ff = pieces[0].shape
    n, s = len(pieces), len(slots)
    cb = divisor(ff, 256)
    steps = ff // cb
    lo, hi = round(steps * SHARES[part]), round(steps * SHARES[part + 1])
    ring = min(RING, hi - lo)
    operands = list(pieces) + ([x for pair in slots for x in pair] if first else [ups, into])

    def body(*refs):
        h, u = refs[:n], refs[n : n + 2 * s] if first else refs[n]
        rest = refs[len(operands) :]
        if first:
            o, ups_ref, out, sent = rest
            c = lax.axis_index("col")
            y, z = lax.rem(c, 2), lax.div(c, 2)
            me = lax.axis_index("dp") * rows + lax.axis_index("row")
            for k in range(s):
                j = lax.bitwise_xor(lax.rem(z + s - k, s), me)
                ups_ref[pl.ds(pl.multiple_of(j * m + y * t, t), t), :] = u[2 * k][...]
                ups_ref[pl.ds(pl.multiple_of(j * m + (1 - y) * t, t), t), :] = u[2 * k + 1][...]
        else:
            o, out, sent = rest
            ups_ref = u

        def store(i):
            slot = lax.rem(i - lo, ring)
            return pltpu.make_async_copy(
                out.at[slot], o.at[pl.ds(pl.multiple_of(i * cb, cb), cb), :], sent.at[slot]
            )

        def step(i, carry):
            @pl.when(i >= lo + ring)
            def _():
                store(i - ring).wait()

            here = pl.ds(pl.multiple_of(i * cb, cb), cb)
            hid = jnp.concatenate([x[:, here] for x in h], axis=0)
            out[lax.rem(i - lo, ring)] = lax.dot_general(
                hid, ups_ref[...], (((0,), (0,)), ((), ())), preferred_element_type=jnp.float32
            )
            store(i).start()
            return carry

        lax.fori_loop(lo, hi, step, 0)
        for i in range(hi - ring, hi):
            store(jnp.int32(i)).wait()

    width = (hi - lo) * cb
    grad = jax.ShapeDtypeStruct((ff, d), jnp.float32)
    everyone = jax.ShapeDtypeStruct((n * m, d), jnp.bfloat16)
    return pl.pallas_call(
        body,
        in_specs=[VMEM] * n + ([VMEM] * (2 * s) if first else [VMEM, HBM]),
        out_specs=[HBM, VMEM] if first else [HBM],
        out_shape=[grad, everyone] if first else [grad],
        input_output_aliases={} if first else {len(operands) - 1: 0},
        scratch_shapes=[pltpu.VMEM((ring, cb, d), jnp.float32), pltpu.SemaphoreType.DMA((ring,))],
        compiler_params=pltpu.CompilerParams(vmem_limit_bytes=GRANT_W << 20),
        cost_estimate=pl.CostEstimate(flops=2 * n * m * d * width, bytes_accessed=4 * d * width, transcendentals=0),
    )(*operands)


def small(body, outs, *args):
    return pl.pallas_call(
        body,
        in_specs=[VMEM] * len(args),
        out_specs=[VMEM] * len(outs),
        out_shape=[jax.ShapeDtypeStruct(o, jnp.bfloat16) for o in outs],
        compiler_params=pltpu.CompilerParams(vmem_limit_bytes=GRANT_S << 20),
        cost_estimate=pl.CostEstimate(flops=2 * args[0].size, bytes_accessed=8 * args[0].size, transcendentals=0),
    )(*args)


def even_is_home(rows):
    return lax.rem(lax.div(lax.axis_index("col"), 2), rows) == lax.axis_index("row")


def wide(x):
    return x.astype(jnp.float32)


def chip_sums(keep, got, rows):
    t = keep.shape[0] // 2

    def body(keep, got, stay, go):
        first = jnp.where(even_is_home(rows), 0, t)
        for out, start in ((stay, first), (go, t - first)):
            at = pl.ds(pl.multiple_of(start, t), t)
            out[...] = (wide(keep[at, :]) + wide(got[at, :])).astype(out.dtype)

    return small(body, [(t, keep.shape[1])] * 2, keep, got)


def finish(stay_a, come_a, stay_b, come_b, rows, blocks):
    def body(stay_a, come_a, stay_b, come_b, kept, give):
        z = lax.div(lax.axis_index("col"), 2)
        slot = jnp.where(even_is_home(rows), 0, 1)
        mine = lax.div(lax.rem(z + blocks - slot, blocks), rows) == lax.axis_index("dp")

        @pl.when(mine)
        def _():
            kept[...] = (wide(stay_a[...]) + wide(come_a[...])).astype(kept.dtype)
            give[...] = (wide(stay_b[...]) + wide(come_b[...])).astype(give.dtype)

        @pl.when(jnp.logical_not(mine))
        def _():
            give[...] = (wide(stay_a[...]) + wide(come_a[...])).astype(kept.dtype)
            kept[...] = (wide(stay_b[...]) + wide(come_b[...])).astype(give.dtype)

    return small(body, [stay_a.shape] * 2, stay_a, come_a, stay_b, come_b)


def joined(kept, got):
    t = kept.shape[0]

    def body(kept, got, o):
        core = lax.axis_index("dp")
        o[pl.ds(pl.multiple_of(core * t, t), t), :] = kept[...]
        o[pl.ds(pl.multiple_of((1 - core) * t, t), t), :] = got[...]

    return small(body, [(2 * t, kept.shape[1])], kept, got)[0]


def blockwise(shape):
    dps, rows, cols = (shape[a] for a in ALL)
    blocks = dps * rows
    swap = [(0, 1), (1, 0)]
    across = [(c, c ^ 1) for c in range(cols)]
    shift = lambda k: [(c, (c + 2 * k) % cols) for c in range(cols)]
    move = lambda x, axis, perm: lax.ppermute(x, axis, perm)

    def local(hidden, upstream, weight):
        far1 = move(upstream, "col", shift(1))
        near0 = move(upstream, "col", across)
        far3 = move(upstream, "col", shift(blocks - 1))
        hidden_x = move(hidden, "row", swap)
        hidden_d = move(hidden, "dp", swap)
        near1 = move(far1, "col", across)
        far2 = move(far1, "col", shift(1))
        near3 = move(far3, "col", across)
        near2 = move(far2, "col", across)
        hidden_xd = move(hidden_x, "dp", swap)
        slots = [(upstream, near0), (far1, near1), (far2, near2), (far3, near3)]
        pieces = [hidden, hidden_x, hidden_d, hidden_xd]

        held = [fetched(weight, i) for i in range(2)]
        keep_a, give_a = block_terms([slots[0], slots[1]], held)
        got_a = move(give_a, "dp", swap)
        stay_a, go_a = chip_sums(keep_a, got_a, rows)
        come_a = move(go_a, "row", swap)
        keep_b, give_b = block_terms([slots[2], slots[3]], held)
        got_b = move(give_b, "dp", swap)
        grad, ups = weight_gradient(pieces, slots, rows, 0, None)
        stay_b, go_b = chip_sums(keep_b, got_b, rows)
        come_b = move(go_b, "row", swap)
        grad, = weight_gradient(pieces, ups, rows, 1, grad)
        kept, give = finish(stay_a, come_a, stay_b, come_b, rows, blocks)
        got = move(give, "dp", swap)
        for p in range(2, len(SHARES) - 1):
            grad, = weight_gradient(pieces, ups, rows, p, grad)
        return joined(kept, got), grad

    return local


def solution(mesh):
    shape = mesh.shape
    fits = shape["dp"] == 2 and shape["row"] == 2 and shape["col"] == 2 * shape["dp"] * shape["row"]
    return jax.shard_map(
        blockwise(shape) if fits else plain,
        mesh=mesh,
        in_specs=(P(TOKENS, "col"), P("col", TOKENS), P("col", TOKENS)),
        out_specs=(P(TOKENS, "col"), P("col", TOKENS)),
        check_vma=False,
    )
```

time: 145 us -> 77.3 us (0.53)
  waiting for transfers between devices: 100 us -> 28.8 us
  Pallas kernels: 0 us -> 33.1 us
  matrix products: 30.1 us -> 0 us
  starting transfers between devices: 0.11 us -> 14.5 us
  between operations: 13.7 us -> 0.77 us
    all_gather x2 -> x0, waiting for transfers between devices: 71.9 us -> none  [the longest x1 53.2 us: local(): gathered = lax.all_gather(upstream, 'col', axis=0, tiled=True)]
    pallas_call x0 -> x11, Pallas kernels: none -> 33.1 us  [the longest x3 14.6 us: weight_gradient(): pl.pallas_call(body, in_specs=[VMEM] * n + ([VMEM] * (2 * s) if first els...]
    dot_general x2 -> x0, matrix products: 30.1 us -> none  [the longest x1 17.2 us: local(): lax.dot_general(lax.all_gather(hidden, ('dp', 'row'), axis=0, tiled=True)...]
    ppermute x0 -> x15, waiting for transfers between devices: none -> 28.8 us  [blockwise(): move = lambda x, axis, perm: lax.ppermute(x, axis, perm)]
    reduce_scatter x1 -> x0, waiting for transfers between devices: 27.2 us -> none  [local(): lax.psum_scatter(lax.dot_general(picked, weight, (((1,), (1,)), ((), ()))...]
    ppermute x0 -> x15, starting transfers between devices: none -> 14.5 us  [blockwise(): move = lambda x, axis, perm: lax.ppermute(x, axis, perm)]
  transfers between devices with their start and end apart: 3 -> 15, of which waited for: 3 -> 8; matrix products, arithmetic and copies ran while one was open for 21% -> 0% of each run, Pallas kernels for 0% -> 41%
where the time goes in v1:
time: 77.3 us; the launch traced here: 77.2 us
  Pallas kernels  33.1 us (43%)
  waiting for transfers between devices  28.8 us (37%)
  starting transfers between devices  14.5 us (19%)
    ppermute x15, waiting for transfers between devices, blockwise(): move = lambda x, axis, perm: lax.ppermute(x, axis, perm)  28.8 us
    pallas_call x3, Pallas kernels, weight_gradient(): pl.pallas_call(body, in_specs=[VMEM] * n + ([VMEM] * (2 * s) if first els...  14.6 us
    ppermute x15, starting transfers between devices, blockwise(): move = lambda x, axis, perm: lax.ppermute(x, axis, perm)  14.5 us
    pallas_call x2, Pallas kernels, block_terms(): pl.pallas_call(body, in_specs=[VMEM] * (2 * n + 2), out_specs=[VMEM] * 2,...  10.4 us
    pallas_call x2, Pallas kernels, fetched(): pl.pallas_call(body, in_specs=[HBM], out_specs=VMEM, out_shape=jax.ShapeD...  6.41 us
    pallas_call x4, Pallas kernels, small(): pl.pallas_call(body, in_specs=[VMEM] * len(args), out_specs=[VMEM] * len(...  1.63 us
  transfers between devices with their start and end apart: 15, of which 8 were waited for; matrix products, arithmetic and copies ran while one was open for 0% of the time, Pallas kernels for 41%

profile of v1, /device:TPU:0, one launch (start us, length us, event | category | flops | bytes accessed | tf_op | source)
XLA Modules:
  0.0 77.2 jit_solution(4238231186528130261)
XLA Ops:
  0.6 3.1 %collective-permute-start.1 = (bf16[64,2048]{1,0:T(8,128)(2,1)}, bf16[64,2048]{1,0:T(8,128)(2,1)S(1)}, u32[]{:S(2)}, u32[]{:S(2)}) collective-permute-start(bf16[64,2048]{1,0:T(8,128)(2,1)} %refs_4_.1), channel_id=1, source_target_pairs={{0,2},{1,3},{2,4},{3,5},{4,6},{5,7},{6,0},{7,1},{8,10},{9,11},{10,... | collective-permute-start | bytes 786440 | tf_op jit(solution)/shard_map/ppermute | solution.py:253
  3.7 2.1 %collective-permute-start.7 = (bf16[64,2048]{1,0:T(8,128)(2,1)}, bf16[64,2048]{1,0:T(8,128)(2,1)S(1)}, u32[]{:S(2)}, u32[]{:S(2)}) collective-permute-start(bf16[64,2048]{1,0:T(8,128)(2,1)} %refs_4_.1), channel_id=1, source_target_pairs={{0,6},{1,7},{2,0},{3,1},{4,2},{5,3},{6,4},{7,5},{8,14},{9,15},{10,... | collective-permute-start | bytes 786440 | tf_op jit(solution)/shard_map/ppermute | solution.py:253
  5.8 7.3 %collective-permute-done.1.refs_2_.refs_6_ = bf16[64,2048]{1,0:T(8,128)(2,1)S(1)} collective-permute-done((bf16[64,2048]{1,0:T(8,128)(2,1)}, bf16[64,2048]{1,0:T(8,128)(2,1)S(1)}, u32[]{:S(2)}, u32[]{:S(2)}) %collective-permute-start.1) | collective-permute-done | bytes 262176 | tf_op jit(solution)/shard_map/ppermute | solution.py:253
  13.2 1.7 %collective-permute-start = (bf16[64,2048]{1,0:T(8,128)(2,1)}, bf16[64,2048]{1,0:T(8,128)(2,1)S(1)}, u32[]{:S(2)}, u32[]{:S(2)}) collective-permute-start(bf16[64,2048]{1,0:T(8,128)(2,1)} %refs_4_.1), channel_id=1, source_target_pairs={{0,1},{1,0},{2,3},{3,2},{4,5},{5,4},{6,7},{7,6},{8,9},{9,8},{10,11... | collective-permute-start | bytes 786440 | tf_op jit(solution)/shard_map/ppermute | solution.py:253
  14.9 0.3 collective-permute-start.2
  15.2 1.7 %collective-permute-start.12 = (bf16[128,3584]{1,0:T(8,128)(2,1)}, bf16[128,3584]{1,0:T(8,128)(2,1)S(1)}, u32[]{:S(2)}, u32[]{:S(2)}) collective-permute-start(bf16[128,3584]{1,0:T(8,128)(2,1)} %refs_0_.7), channel_id=1, source_target_pairs={{0,8},{8,0},{1,9},{9,1},{2,10},{10,2},{3,11},{11,3},{4,12},{12,4},... | collective-permute-start | bytes 2752520 | tf_op jit(solution)/shard_map/ppermute | solution.py:253
  16.9 3.2 %shard_map.51.refs_5_ = bf16[1792,2048]{1,0:T(8,128)(2,1)S(1)} custom-call(bf16[3584,2048]{1,0:T(8,128)(2,1)} %w.3), custom_call_target="tpu_custom_call" | custom-call | flops 3670016 | bytes 7340032 | tf_op jit(solution)/shard_map/pallas_call | solution.py:70
  20.1 3.2 %shard_map.50.refs_4_ = bf16[1792,2048]{1,0:T(8,128)(2,1)S(1)} custom-call(bf16[3584,2048]{1,0:T(8,128)(2,1)} %w.3), custom_call_target="tpu_custom_call" | custom-call | flops 3670016 | bytes 7340032 | tf_op jit(solution)/shard_map/pallas_call | solution.py:70
  23.4 1.6 %collective-permute-start.8 = (bf16[64,2048]{1,0:T(8,128)(2,1)S(1)}, bf16[64,2048]{1,0:T(8,128)(2,1)S(1)}, u32[]{:S(2)}, u32[]{:S(2)}) collective-permute-start(bf16[64,2048]{1,0:T(8,128)(2,1)S(1)} %collective-permute-done.7.refs_2_.refs_10_), channel_id=1, source_target_pairs={{0,1},{1,0},{2,3},{3,2},{4,5},{5,4},{6,7},{7,6},{8,9},{9,8},{10,11... | collective-permute-start | bytes 786440 | tf_op jit(solution)/shard_map/ppermute | solution.py:253
  25.0 0.5 collective-permute-start.6
  25.5 2.6 %collective-permute-done.2.refs_3_.refs_7_ = bf16[64,2048]{1,0:T(8,128)(2,1)S(1)} collective-permute-done((bf16[64,2048]{1,0:T(8,128)(2,1)S(1)}, bf16[64,2048]{1,0:T(8,128)(2,1)S(1)}, u32[]{:S(2)}, u32[]{:S(2)}) %collective-permute-start.2) | collective-permute-done | bytes 262176 | tf_op jit(solution)/shard_map/ppermute | solution.py:253
  28.1 5.2 %shard_map.52 = (bf16[128,3584]{1,0:T(8,128)(2,1)S(1)}, bf16[128,3584]{1,0:T(8,128)(2,1)S(1)}) custom-call(bf16[64,2048]{1,0:T(8,128)(2,1)S(1)} %copy-done.1, bf16[64,2048]{1,0:T(8,128)(2,1)S(1)} %collective-permute-done.refs_1_.refs_5_, bf16[64,2048]{1,0:T(8,128)(2,1)S(1)} %collective-permute-done.1.refs_2_.refs_6_, ...), custom_call_target="tpu_custom_call" | custom-call | flops 3758096384 | bytes 14680064 | tf_op jit(solution)/shard_map/pallas_call | solution.py:109
  33.3 0.1 collective-permute-start.3
  33.4 0.3 collective-permute-done.8.refs_3_.refs_11_
  33.7 3.2 %collective-permute-done.6.refs_1_.refs_9_ = bf16[64,2048]{1,0:T(8,128)(2,1)S(1)} collective-permute-done((bf16[64,2048]{1,0:T(8,128)(2,1)S(1)}, bf16[64,2048]{1,0:T(8,128)(2,1)S(1)}, u32[]{:S(2)}, u32[]{:S(2)}) %collective-permute-start.6) | collective-permute-done | bytes 262176 | tf_op jit(solution)/shard_map/ppermute | solution.py:253
  36.9 5.2 %shard_map.54 = (bf16[128,3584]{1,0:T(8,128)(2,1)S(1)}, bf16[128,3584]{1,0:T(8,128)(2,1)S(1)}) custom-call(bf16[64,2048]{1,0:T(8,128)(2,1)S(1)} %collective-permute-done.5.refs_0_.refs_8_, bf16[64,2048]{1,0:T(8,128)(2,1)S(1)} %collective-permute-done.6.refs_1_.refs_9_, bf16[64,2048]{1,0:T(8,128)(2,1)S(1)} %collective-permute-done.7.refs_2_.refs_10_, ...), custom_call_target="tpu_custom_call" | custom-call | flops 3758096384 | bytes 14680064 | tf_op jit(solution)/shard_map/pallas_call | solution.py:109
  42.1 0.1 collective-permute-start.9
  42.2 0.5 collective-permute-start.13
  42.7 0.1 collective-permute-start.14
  42.7 0.2 shard_map.53
  43.0 1.3 %collective-permute-start.4 = (bf16[64,3584]{1,0:T(8,128)(2,1)S(1)}, bf16[64,3584]{1,0:T(8,128)(2,1)S(1)}, u32[]{:S(2)}, u32[]{:S(2)}) collective-permute-start(bf16[64,3584]{1,0:T(8,128)(2,1)S(1)} %get-tuple-element.17), channel_id=1, source_target_pairs={{0,8},{8,0},{1,9},{9,1},{2,10},{10,2},{3,11},{11,3},{4,12},{12,4},... | collective-permute-start | bytes 1376264 | tf_op jit(solution)/shard_map/ppermute | solution.py:253
  44.3 0.3 collective-permute-done.9.got
  44.6 0.2 shard_map.55
  44.8 1.3 %collective-permute-start.10 = (bf16[64,3584]{1,0:T(8,128)(2,1)S(1)}, bf16[64,3584]{1,0:T(8,128)(2,1)S(1)}, u32[]{:S(2)}, u32[]{:S(2)}) collective-permute-start(bf16[64,3584]{1,0:T(8,128)(2,1)S(1)} %get-tuple-element.21), channel_id=1, source_target_pairs={{0,8},{8,0},{1,9},{9,1},{2,10},{10,2},{3,11},{11,3},{4,12},{12,4},... | collective-permute-start | bytes 1376264 | tf_op jit(solution)/shard_map/ppermute | solution.py:253
  46.2 1.1 %collective-permute-done.14.refs_3_ = bf16[128,3584]{1,0:T(8,128)(2,1)S(1)} collective-permute-done((bf16[128,3584]{1,0:T(8,128)(2,1)S(1)}, bf16[128,3584]{1,0:T(8,128)(2,1)S(1)}, u32[]{:S(2)}, u32[]{:S(2)}) %collective-permute-start.14) | collective-permute-done | bytes 917536 | tf_op jit(solution)/shard_map/ppermute | solution.py:253
  47.2 4.5 %shard_map.58 = (f32[3584,2048]{1,0:T(8,128)}, bf16[512,2048]{1,0:T(8,128)(2,1)S(1)}) custom-call(bf16[128,3584]{1,0:T(8,128)(2,1)S(1)} %copy-done, bf16[128,3584]{1,0:T(8,128)(2,1)S(1)} %collective-permute-done.12.refs_1_, bf16[128,3584]{1,0:T(8,128)(2,1)S(1)} %collective-permute-done.13.refs_2_, bf16[128,3584]{1,0:T(8,128)(2,1)S(1)} %collective-permute-done.14.refs_3_, ...), custom_call_target="tpu_custom_call" | custom-call | flops 2147483648 | bytes 8388608 | tf_op jit(solution)/shard_map/pallas_call | solution.py:174
  51.7 4.7 %collective-permute-done.4.come_a = bf16[64,3584]{1,0:T(8,128)(2,1)S(1)} collective-permute-done((bf16[64,3584]{1,0:T(8,128)(2,1)S(1)}, bf16[64,3584]{1,0:T(8,128)(2,1)S(1)}, u32[]{:S(2)}, u32[]{:S(2)}) %collective-permute-start.4) | collective-permute-done | bytes 458784 | tf_op jit(solution)/shard_map/ppermute | solution.py:253
  56.4 9.3 %collective-permute-done.10.come_b = bf16[64,3584]{1,0:T(8,128)(2,1)S(1)} collective-permute-done((bf16[64,3584]{1,0:T(8,128)(2,1)S(1)}, bf16[64,3584]{1,0:T(8,128)(2,1)S(1)}, u32[]{:S(2)}, u32[]{:S(2)}) %collective-permute-start.10) | collective-permute-done | bytes 458784 | tf_op jit(solution)/shard_map/ppermute | solution.py:253
  65.7 0.2 shard_map.56
  66.0 5.8 %shard_map.59.refs_5_ = f32[3584,2048]{1,0:T(8,128)} custom-call(bf16[128,3584]{1,0:T(8,128)(2,1)S(1)} %copy-done, bf16[128,3584]{1,0:T(8,128)(2,1)S(1)} %collective-permute-done.12.refs_1_, bf16[128,3584]{1,0:T(8,128)(2,1)S(1)} %collective-permute-done.13.refs_2_, ...), custom_call_target="tpu_custom_call", output_to_operand_aliasing={{}: (5, {})} | custom-call | flops 3221225472 | bytes 12582912 | tf_op jit(solution)/shard_map/pallas_call | solution.py:174
  71.8 4.3 %shard_map.60 = f32[3584,2048]{1,0:T(8,128)} custom-call(bf16[128,3584]{1,0:T(8,128)(2,1)S(1)} %copy-done, bf16[128,3584]{1,0:T(8,128)(2,1)S(1)} %collective-permute-done.12.refs_1_, bf16[128,3584]{1,0:T(8,128)(2,1)S(1)} %collective-permute-done.13.refs_2_, bf16[128,3584]{1,0:T(8,128)(2,1)S(1)} %collective-permute-done.14.refs_3_, ...), custom_call_target="tpu_custom_call", output_to_operand_aliasing={{}: (5, {})} | custom-call | flops 2147483648 | bytes 8388608 | tf_op jit(solution)/shard_map/pallas_call | solution.py:174
  76.2 1.0 %shard_map.57 = bf16[128,3584]{1,0:T(8,128)(2,1)} custom-call(bf16[64,3584]{1,0:T(8,128)(2,1)S(1)} %get-tuple-element.22.kept, bf16[64,3584]{1,0:T(8,128)(2,1)S(1)} %collective-permute-done.11.got), custom_call_target="tpu_custom_call" | custom-call | flops 458752 | bytes 1835008 | tf_op jit(solution)/shard_map/pallas_call | solution.py:187
  (13 shorter events, 0.1 us)
Async XLA Ops:
  0.6 12.5 %collective-permute-start.1 = (bf16[64,2048]{1,0:T(8,128)(2,1)}, bf16[64,2048]{1,0:T(8,128)(2,1)S(1)}, u32[]{:S(2)}, u32[]{:S(2)}) collective-permute-start(bf16[64,2048]{1,0:T(8,128)(2,1)} %refs_4_.1), channel_id=1, source_target_pairs={{0,2},{1,3},{2,4},{3,5},{4,6},{5,7},{6,0},{7,1},{8,10},{9,11},{10,... | collective-permute-start | bytes 786440 | tf_op jit(solution)/shard_map/ppermute | solution.py:253
  3.7 19.6 %collective-permute-start.7 = (bf16[64,2048]{1,0:T(8,128)(2,1)}, bf16[64,2048]{1,0:T(8,128)(2,1)S(1)}, u32[]{:S(2)}, u32[]{:S(2)}) collective-permute-start(bf16[64,2048]{1,0:T(8,128)(2,1)} %refs_4_.1), channel_id=1, source_target_pairs={{0,6},{1,7},{2,0},{3,1},{4,2},{5,3},{6,4},{7,5},{8,14},{9,15},{10,... | collective-permute-start | bytes 786440 | tf_op jit(solution)/shard_map/ppermute | solution.py:253
  13.2 11.8 %collective-permute-start.5 = (bf16[64,2048]{1,0:T(8,128)(2,1)S(1)}, bf16[64,2048]{1,0:T(8,128)(2,1)S(1)}, u32[]{:S(2)}, u32[]{:S(2)}) collective-permute-start(bf16[64,2048]{1,0:T(8,128)(2,1)S(1)} %collective-permute-done.1.refs_2_.refs_6_), channel_id=1, source_target_pairs={{0,2},{1,3},{2,4},{3,5},{4,6},{5,7},{6,0},{7,1},{8,10},{9,11},{10,... | collective-permute-start | bytes 786440 | tf_op jit(solution)/shard_map/ppermute | solution.py:253
  13.2 12.3 %collective-permute-start = (bf16[64,2048]{1,0:T(8,128)(2,1)}, bf16[64,2048]{1,0:T(8,128)(2,1)S(1)}, u32[]{:S(2)}, u32[]{:S(2)}) collective-permute-start(bf16[64,2048]{1,0:T(8,128)(2,1)} %refs_4_.1), channel_id=1, source_target_pairs={{0,1},{1,0},{2,3},{3,2},{4,5},{5,4},{6,7},{7,6},{8,9},{9,8},{10,11... | collective-permute-start | bytes 786440 | tf_op jit(solution)/shard_map/ppermute | solution.py:253
  14.9 13.2 %collective-permute-start.2 = (bf16[64,2048]{1,0:T(8,128)(2,1)S(1)}, bf16[64,2048]{1,0:T(8,128)(2,1)S(1)}, u32[]{:S(2)}, u32[]{:S(2)}) collective-permute-start(bf16[64,2048]{1,0:T(8,128)(2,1)S(1)} %collective-permute-done.1.refs_2_.refs_6_), channel_id=1, source_target_pairs={{0,1},{1,0},{2,3},{3,2},{4,5},{5,4},{6,7},{7,6},{8,9},{9,8},{10,11... | collective-permute-start | bytes 786440 | tf_op jit(solution)/shard_map/ppermute | solution.py:253
  15.2 27.5 %collective-permute-start.12 = (bf16[128,3584]{1,0:T(8,128)(2,1)}, bf16[128,3584]{1,0:T(8,128)(2,1)S(1)}, u32[]{:S(2)}, u32[]{:S(2)}) collective-permute-start(bf16[128,3584]{1,0:T(8,128)(2,1)} %refs_0_.7), channel_id=1, source_target_pairs={{0,8},{8,0},{1,9},{9,1},{2,10},{10,2},{3,11},{11,3},{4,12},{12,4},... | collective-permute-start | bytes 2752520 | tf_op jit(solution)/shard_map/ppermute | solution.py:253
  20.1 8.0 %copy-start.1 = (bf16[64,2048]{1,0:T(8,128)(2,1)S(1)}, bf16[64,2048]{1,0:T(8,128)(2,1)}, u32[]{:S(2)}) copy-start(bf16[64,2048]{1,0:T(8,128)(2,1)} %refs_4_.1) | copy-start | bytes 786436
  23.3 18.8 %copy-start = (bf16[128,3584]{1,0:T(8,128)(2,1)S(1)}, bf16[128,3584]{1,0:T(8,128)(2,1)}, u32[]{:S(2)}) copy-start(bf16[128,3584]{1,0:T(8,128)(2,1)} %refs_0_.7) | copy-start | bytes 2752516
  23.4 10.3 %collective-permute-start.8 = (bf16[64,2048]{1,0:T(8,128)(2,1)S(1)}, bf16[64,2048]{1,0:T(8,128)(2,1)S(1)}, u32[]{:S(2)}, u32[]{:S(2)}) collective-permute-start(bf16[64,2048]{1,0:T(8,128)(2,1)S(1)} %collective-permute-done.7.refs_2_.refs_10_), channel_id=1, source_target_pairs={{0,1},{1,0},{2,3},{3,2},{4,5},{5,4},{6,7},{7,6},{8,9},{9,8},{10,11... | collective-permute-start | bytes 786440 | tf_op jit(solution)/shard_map/ppermute | solution.py:253
  25.0 11.9 %collective-permute-start.6 = (bf16[64,2048]{1,0:T(8,128)(2,1)S(1)}, bf16[64,2048]{1,0:T(8,128)(2,1)S(1)}, u32[]{:S(2)}, u32[]{:S(2)}) collective-permute-start(bf16[64,2048]{1,0:T(8,128)(2,1)S(1)} %collective-permute-done.5.refs_0_.refs_8_), channel_id=1, source_target_pairs={{0,1},{1,0},{2,3},{3,2},{4,5},{5,4},{6,7},{7,6},{8,9},{9,8},{10,11... | collective-permute-start | bytes 786440 | tf_op jit(solution)/shard_map/ppermute | solution.py:253
  33.3 9.4 %collective-permute-start.3 = (bf16[128,3584]{1,0:T(8,128)(2,1)S(1)}, bf16[128,3584]{1,0:T(8,128)(2,1)S(1)}, u32[]{:S(2)}, u32[]{:S(2)}) collective-permute-start(bf16[128,3584]{1,0:T(8,128)(2,1)S(1)} %get-tuple-element.15), channel_id=1, source_target_pairs={{0,16},{16,0},{1,17},{17,1},{2,18},{18,2},{3,19},{19,3},{4,20},{20... | collective-permute-start | bytes 2752520 | tf_op jit(solution)/shard_map/ppermute | solution.py:253
  42.1 2.5 %collective-permute-start.9 = (bf16[128,3584]{1,0:T(8,128)(2,1)S(1)}, bf16[128,3584]{1,0:T(8,128)(2,1)S(1)}, u32[]{:S(2)}, u32[]{:S(2)}) collective-permute-start(bf16[128,3584]{1,0:T(8,128)(2,1)S(1)} %get-tuple-element.19), channel_id=1, source_target_pairs={{0,16},{16,0},{1,17},{17,1},{2,18},{18,2},{3,19},{19,3},{4,20},{20... | collective-permute-start | bytes 2752520 | tf_op jit(solution)/shard_map/ppermute | solution.py:253
  42.2 4.0 %collective-permute-start.13 = (bf16[128,3584]{1,0:T(8,128)(2,1)S(1)}, bf16[128,3584]{1,0:T(8,128)(2,1)S(1)}, u32[]{:S(2)}, u32[]{:S(2)}) collective-permute-start(bf16[128,3584]{1,0:T(8,128)(2,1)S(1)} %copy-done), channel_id=1, source_target_pairs={{0,16},{16,0},{1,17},{17,1},{2,18},{18,2},{3,19},{19,3},{4,20},{20... | collective-permute-start | bytes 2752520 | tf_op jit(solution)/shard_map/ppermute | solution.py:253
  42.7 4.6 %collective-permute-start.14 = (bf16[128,3584]{1,0:T(8,128)(2,1)S(1)}, bf16[128,3584]{1,0:T(8,128)(2,1)S(1)}, u32[]{:S(2)}, u32[]{:S(2)}) collective-permute-start(bf16[128,3584]{1,0:T(8,128)(2,1)S(1)} %collective-permute-done.12.refs_1_), channel_id=1, source_target_pairs={{0,16},{16,0},{1,17},{17,1},{2,18},{18,2},{3,19},{19,3},{4,20},{20... | collective-permute-start | bytes 2752520 | tf_op jit(solution)/shard_map/ppermute | solution.py:253
  43.0 13.5 %collective-permute-start.4 = (bf16[64,3584]{1,0:T(8,128)(2,1)S(1)}, bf16[64,3584]{1,0:T(8,128)(2,1)S(1)}, u32[]{:S(2)}, u32[]{:S(2)}) collective-permute-start(bf16[64,3584]{1,0:T(8,128)(2,1)S(1)} %get-tuple-element.17), channel_id=1, source_target_pairs={{0,8},{8,0},{1,9},{9,1},{2,10},{10,2},{3,11},{11,3},{4,12},{12,4},... | collective-permute-start | bytes 1376264 | tf_op jit(solution)/shard_map/ppermute | solution.py:253
  44.8 20.9 %collective-permute-start.10 = (bf16[64,3584]{1,0:T(8,128)(2,1)S(1)}, bf16[64,3584]{1,0:T(8,128)(2,1)S(1)}, u32[]{:S(2)}, u32[]{:S(2)}) collective-permute-start(bf16[64,3584]{1,0:T(8,128)(2,1)S(1)} %get-tuple-element.21), channel_id=1, source_target_pairs={{0,8},{8,0},{1,9},{9,1},{2,10},{10,2},{3,11},{11,3},{4,12},{12,4},... | collective-permute-start | bytes 1376264 | tf_op jit(solution)/shard_map/ppermute | solution.py:253
  65.9 10.2 %collective-permute-start.11 = (bf16[64,3584]{1,0:T(8,128)(2,1)S(1)}, bf16[64,3584]{1,0:T(8,128)(2,1)S(1)}, u32[]{:S(2)}, u32[]{:S(2)}) collective-permute-start(bf16[64,3584]{1,0:T(8,128)(2,1)S(1)} %get-tuple-element.23), channel_id=1, source_target_pairs={{0,16},{16,0},{1,17},{17,1},{2,18},{18,2},{3,19},{19,3},{4,20},{20... | collective-permute-start | bytes 1376264 | tf_op jit(solution)/shard_map/ppermute | solution.py:253

commit v2 on v1

--- a/solution.py
+++ b/solution.py
@@ -6,10 +6,10 @@
 from jax.sharding import PartitionSpec as P
 
 
-SHARES = (0, 0.3, 0.75, 1)
-RING = 4
-GRANT_T = 12
-GRANT_W = 20
+SHARES = (0, 0.929, 1)
+RING = 6
+GRANT_T = 16
+GRANT_W = 24
 GRANT_S = 6
 FETCHES = 4
 TOKENS = ("dp", "row")
@@ -81,15 +81,15 @@
 def block_terms(slots, weights):
     t, d = slots[0][0].shape
     half = weights[0].shape[0]
-    n = len(slots)
-    cb = divisor(half, 896)
+    n, parts = len(slots), len(weights)
+    cb = divisor(half, 1792)
     steps = half // cb
 
     def body(*refs):
-        u, w = refs[: 2 * n], refs[2 * n : 2 * n + 2]
-        keep, give, ups = refs[2 * n + 2 :]
+        u, w = refs[: 2 * n], refs[2 * n : 2 * n + parts]
+        keep, give, ups = refs[2 * n + parts :]
         halves(u, ups, t)
-        for h in range(2):
+        for h in range(parts):
 
             def step(i, carry):
                 term = lax.dot_general(
@@ -105,15 +105,15 @@
 
             lax.fori_loop(0, steps, step, 0)
 
-    out = jax.ShapeDtypeStruct((n * t, 2 * half), jnp.bfloat16)
+    out = jax.ShapeDtypeStruct((n * t, parts * half), jnp.bfloat16)
     return pl.pallas_call(
         body,
-        in_specs=[VMEM] * (2 * n + 2),
+        in_specs=[VMEM] * (2 * n + parts),
         out_specs=[VMEM] * 2,
         out_shape=[out, out],
         scratch_shapes=[pltpu.VMEM((2 * n * t, d), jnp.bfloat16)],
         compiler_params=pltpu.CompilerParams(vmem_limit_bytes=GRANT_T << 20),
-        cost_estimate=pl.CostEstimate(flops=8 * n * t * d * half, bytes_accessed=4 * d * half, transcendentals=0),
+        cost_estimate=pl.CostEstimate(flops=4 * n * t * d * half * parts, bytes_accessed=2 * d * half * parts, transcendentals=0),
     )(*[x for pair in slots for x in pair], *weights)
 
 
@@ -146,27 +146,27 @@
             ups_ref = u
 
         def store(i):
-            slot = lax.rem(i - lo, ring)
+            slot = (i - lo) % ring
             return pltpu.make_async_copy(
-                out.at[slot], o.at[pl.ds(pl.multiple_of(i * cb, cb), cb), :], sent.at[slot]
+                out.at[slot], o.at[pl.ds(i * cb, cb), :], sent.at[slot]
             )
 
         def step(i, carry):
-            @pl.when(i >= lo + ring)
-            def _():
+            if i >= lo + ring:
                 store(i - ring).wait()
 
-            here = pl.ds(pl.multiple_of(i * cb, cb), cb)
+            here = pl.ds(i * cb, cb)
             hid = jnp.concatenate([x[:, here] for x in h], axis=0)
-            out[lax.rem(i - lo, ring)] = lax.dot_general(
+            out[(i - lo) % ring] = lax.dot_general(
                 hid, ups_ref[...], (((0,), (0,)), ((), ())), preferred_element_type=jnp.float32
             )
             store(i).start()
             return carry
 
-        lax.fori_loop(lo, hi, step, 0)
+        for i in range(lo, hi):
+            step(i, 0)
         for i in range(hi - ring, hi):
-            store(jnp.int32(i)).wait()
+            store(i).wait()
 
     width = (hi - lo) * cb
     grad = jax.ShapeDtypeStruct((ff, d), jnp.float32)
@@ -215,22 +215,36 @@
 
 
 def finish(stay_a, come_a, stay_b, come_b, rows, blocks):
-    def body(stay_a, come_a, stay_b, come_b, kept, give):
+    sizes = [len(stay_a), len(stay_b)]
+
+    def body(*refs):
+        kept, give = refs[-2:]
         z = lax.div(lax.axis_index("col"), 2)
         slot = jnp.where(even_is_home(rows), 0, 1)
         mine = lax.div(lax.rem(z + blocks - slot, blocks), rows) == lax.axis_index("dp")
 
+        def fill(out, parts):
+            at = 0
+            for i in range(len(parts) // 2):
+                width = parts[i].shape[1]
+                total = wide(parts[i][...]) + wide(parts[i + len(parts) // 2][...])
+                out[:, at : at + width] = total.astype(out.dtype)
+                at += width
+
+        a, b = refs[: 2 * sizes[0]], refs[2 * sizes[0] : -2]
+
         @pl.when(mine)
         def _():
-            kept[...] = (wide(stay_a[...]) + wide(come_a[...])).astype(kept.dtype)
-            give[...] = (wide(stay_b[...]) + wide(come_b[...])).astype(give.dtype)
+            fill(kept, a)
+            fill(give, b)
 
         @pl.when(jnp.logical_not(mine))
         def _():
-            give[...] = (wide(stay_a[...]) + wide(come_a[...])).astype(kept.dtype)
-            kept[...] = (wide(stay_b[...]) + wide(come_b[...])).astype(give.dtype)
-
-    return small(body, [stay_a.shape] * 2, stay_a, come_a, stay_b, come_b)
+            fill(give, a)
+            fill(kept, b)
+
+    shape = (stay_a[0].shape[0], sum(x.shape[1] for x in stay_a))
+    return small(body, [shape] * 2, *stay_a, *come_a, *stay_b, *come_b)
 
 
 def joined(kept, got):
@@ -261,25 +275,31 @@
         near1 = move(far1, "col", across)
         far2 = move(far1, "col", shift(1))
         near3 = move(far3, "col", across)
-        near2 = move(far2, "col", across)
+        near2 = move(near1, "col", shift(1))
         hidden_xd = move(hidden_x, "dp", swap)
         slots = [(upstream, near0), (far1, near1), (far2, near2), (far3, near3)]
         pieces = [hidden, hidden_x, hidden_d, hidden_xd]
 
         held = [fetched(weight, i) for i in range(2)]
-        keep_a, give_a = block_terms([slots[0], slots[1]], held)
-        got_a = move(give_a, "dp", swap)
-        stay_a, go_a = chip_sums(keep_a, got_a, rows)
-        come_a = move(go_a, "row", swap)
-        keep_b, give_b = block_terms([slots[2], slots[3]], held)
-        got_b = move(give_b, "dp", swap)
+
+        def exchanged(pair):
+            stay, come, keeps, gots = [], [], [], []
+            for i in range(2):
+                keep, give = block_terms(pair, held[i : i + 1])
+                keeps.append(keep)
+                gots.append(move(give, "dp", swap))
+            for i in range(2):
+                near, go = chip_sums(keeps[i], gots[i], rows)
+                stay.append(near)
+                come.append(move(go, "row", swap))
+            return stay, come
+
+        stay_a, come_a = exchanged([slots[0], slots[1]])
+        stay_b, come_b = exchanged([slots[2], slots[3]])
         grad, ups = weight_gradient(pieces, slots, rows, 0, None)
-        stay_b, go_b = chip_sums(keep_b, got_b, rows)
-        come_b = move(go_b, "row", swap)
-        grad, = weight_gradient(pieces, ups, rows, 1, grad)
         kept, give = finish(stay_a, come_a, stay_b, come_b, rows, blocks)
         got = move(give, "dp", swap)
-        for p in range(2, len(SHARES) - 1):
+        for p in range(1, len(SHARES) - 1):
             grad, = weight_gradient(pieces, ups, rows, p, grad)
         return joined(kept, got), grad
 

time: 77.3 us -> 78 us (level)
  starting transfers between devices: 14.5 us -> 21.1 us
  Pallas kernels: 33.1 us -> 29.3 us
  waiting for transfers between devices: 28.8 us -> 26.6 us
    ppermute x15 -> x19, starting transfers between devices: 14.5 us -> 21.1 us  [blockwise(): move = lambda x, axis, perm: lax.ppermute(x, axis, perm)]
    pallas_call x3 -> x2, Pallas kernels: 14.6 us -> 12.2 us  [weight_gradient(): pl.pallas_call(body, in_specs=[VMEM] * n + ([VMEM] * (2 * s) if first els...]
    ppermute x15 -> x19, waiting for transfers between devices: 28.8 us -> 26.6 us  [blockwise(): move = lambda x, axis, perm: lax.ppermute(x, axis, perm)]
    pallas_call x2 -> x4, Pallas kernels: 10.4 us -> 8.81 us  [block_terms(): pl.pallas_call(body, in_specs=[VMEM] * (2 * n + parts), out_specs=[VMEM]...]
    pallas_call x4 -> x6, Pallas kernels: 1.63 us -> 1.82 us  [small(): pl.pallas_call(body, in_specs=[VMEM] * len(args), out_specs=[VMEM] * len(...]
  transfers between devices with their start and end apart: 15 -> 19, of which waited for: 8 -> 6; matrix products, arithmetic and copies ran while one was open for 0% -> 0% of each run, Pallas kernels for 41% -> 36%
where the time goes in v2:
time: 78 us; the launch traced here: 77.8 us
  Pallas kernels  29.3 us (38%)
  waiting for transfers between devices  26.6 us (34%)
  starting transfers between devices  21.1 us (27%)
  between operations  0.85 us (1%)
    ppermute x19, waiting for transfers between devices, blockwise(): move = lambda x, axis, perm: lax.ppermute(x, axis, perm)  26.6 us
    ppermute x19, starting transfers between devices, blockwise(): move = lambda x, axis, perm: lax.ppermute(x, axis, perm)  21.1 us
    pallas_call x2, Pallas kernels, weight_gradient(): pl.pallas_call(body, in_specs=[VMEM] * n + ([VMEM] * (2 * s) if first els...  12.2 us
    pallas_call x4, Pallas kernels, block_terms(): pl.pallas_call(body, in_specs=[VMEM] * (2 * n + parts), out_specs=[VMEM]...  8.81 us
    pallas_call x2, Pallas kernels, fetched(): pl.pallas_call(body, in_specs=[HBM], out_specs=VMEM, out_shape=jax.ShapeD...  6.46 us
    pallas_call x6, Pallas kernels, small(): pl.pallas_call(body, in_specs=[VMEM] * len(args), out_specs=[VMEM] * len(...  1.82 us
  transfers between devices with their start and end apart: 19, of which 6 were waited for; matrix products, arithmetic and copies ran while one was open for 0% of the time, Pallas kernels for 36%

profile of v2, /device:TPU:0, one launch (start us, length us, event | category | flops | bytes accessed | tf_op | source)
XLA Modules:
  0.0 77.8 jit_solution(7609186832027982245)
XLA Ops:
  0.6 3.0 %collective-permute-start.16 = (bf16[128,3584]{1,0:T(8,128)(2,1)}, bf16[128,3584]{1,0:T(8,128)(2,1)S(1)}, u32[]{:S(2)}, u32[]{:S(2)}) collective-permute-start(bf16[128,3584]{1,0:T(8,128)(2,1)} %refs_0_.7), channel_id=1, source_target_pairs={{0,8},{8,0},{1,9},{9,1},{2,10},{10,2},{3,11},{11,3},{4,12},{12,4},... | collective-permute-start | bytes 2752520 | tf_op jit(solution)/shard_map/ppermute | solution.py:267
  3.7 1.6 %collective-permute-start.1 = (bf16[64,2048]{1,0:T(8,128)(2,1)}, bf16[64,2048]{1,0:T(8,128)(2,1)S(1)}, u32[]{:S(2)}, u32[]{:S(2)}) collective-permute-start(bf16[64,2048]{1,0:T(8,128)(2,1)} %refs_4_.1), channel_id=1, source_target_pairs={{0,2},{1,3},{2,4},{3,5},{4,6},{5,7},{6,0},{7,1},{8,10},{9,11},{10,... | collective-permute-start | bytes 786440 | tf_op jit(solution)/shard_map/ppermute | solution.py:267
  5.2 2.2 %collective-permute-start.9 = (bf16[64,2048]{1,0:T(8,128)(2,1)}, bf16[64,2048]{1,0:T(8,128)(2,1)S(1)}, u32[]{:S(2)}, u32[]{:S(2)}) collective-permute-start(bf16[64,2048]{1,0:T(8,128)(2,1)} %refs_4_.1), channel_id=1, source_target_pairs={{0,6},{1,7},{2,0},{3,1},{4,2},{5,3},{6,4},{7,5},{8,14},{9,15},{10,... | collective-permute-start | bytes 786440 | tf_op jit(solution)/shard_map/ppermute | solution.py:267
  7.5 7.4 %collective-permute-done.1.refs_2_.refs_6_ = bf16[64,2048]{1,0:T(8,128)(2,1)S(1)} collective-permute-done((bf16[64,2048]{1,0:T(8,128)(2,1)}, bf16[64,2048]{1,0:T(8,128)(2,1)S(1)}, u32[]{:S(2)}, u32[]{:S(2)}) %collective-permute-start.1) | collective-permute-done | bytes 262176 | tf_op jit(solution)/shard_map/ppermute | solution.py:267
  14.9 1.5 %collective-permute-start.2 = (bf16[64,2048]{1,0:T(8,128)(2,1)S(1)}, bf16[64,2048]{1,0:T(8,128)(2,1)S(1)}, u32[]{:S(2)}, u32[]{:S(2)}) collective-permute-start(bf16[64,2048]{1,0:T(8,128)(2,1)S(1)} %collective-permute-done.1.refs_2_.refs_6_), channel_id=1, source_target_pairs={{0,1},{1,0},{2,3},{3,2},{4,5},{5,4},{6,7},{7,6},{8,9},{9,8},{10,11... | collective-permute-start | bytes 786440 | tf_op jit(solution)/shard_map/ppermute | solution.py:267
  16.4 0.5 collective-permute-start
  16.9 3.2 %shard_map.53.refs_4_ = bf16[1792,2048]{1,0:T(8,128)(2,1)S(1)} custom-call(bf16[3584,2048]{1,0:T(8,128)(2,1)} %w.3), custom_call_target="tpu_custom_call" | custom-call | flops 3670016 | bytes 7340032 | tf_op jit(solution)/shard_map/pallas_call | solution.py:70
  20.1 3.3 %shard_map.50.refs_4_ = bf16[1792,2048]{1,0:T(8,128)(2,1)S(1)} custom-call(bf16[3584,2048]{1,0:T(8,128)(2,1)} %w.3), custom_call_target="tpu_custom_call" | custom-call | flops 3670016 | bytes 7340032 | tf_op jit(solution)/shard_map/pallas_call | solution.py:70
  23.5 1.6 %collective-permute-start.10 = (bf16[64,2048]{1,0:T(8,128)(2,1)S(1)}, bf16[64,2048]{1,0:T(8,128)(2,1)S(1)}, u32[]{:S(2)}, u32[]{:S(2)}) collective-permute-start(bf16[64,2048]{1,0:T(8,128)(2,1)S(1)} %collective-permute-done.9.refs_2_.refs_10_), channel_id=1, source_target_pairs={{0,1},{1,0},{2,3},{3,2},{4,5},{5,4},{6,7},{7,6},{8,9},{9,8},{10,11... | collective-permute-start | bytes 786440 | tf_op jit(solution)/shard_map/ppermute | solution.py:267
  25.1 5.4 %collective-permute-start.8 = (bf16[64,2048]{1,0:T(8,128)(2,1)S(1)}, bf16[64,2048]{1,0:T(8,128)(2,1)S(1)}, u32[]{:S(2)}, u32[]{:S(2)}) collective-permute-start(bf16[64,2048]{1,0:T(8,128)(2,1)S(1)} %collective-permute-done.2.refs_3_.refs_7_), channel_id=1, source_target_pairs={{0,2},{1,3},{2,4},{3,5},{4,6},{5,7},{6,0},{7,1},{8,10},{9,11},{10,... | collective-permute-start | bytes 786440 | tf_op jit(solution)/shard_map/ppermute | solution.py:267
  30.5 2.2 %shard_map.54 = (bf16[128,1792]{1,0:T(8,128)(2,1)S(1)}, bf16[128,1792]{1,0:T(8,128)(2,1)S(1)}) custom-call(bf16[64,2048]{1,0:T(8,128)(2,1)S(1)} %copy-done, bf16[64,2048]{1,0:T(8,128)(2,1)S(1)} %collective-permute-done.refs_1_.refs_5_, bf16[64,2048]{1,0:T(8,128)(2,1)S(1)} %collective-permute-done.1.refs_2_.refs_6_, ...), custom_call_target="tpu_custom_call" | custom-call | flops 1879048192 | bytes 7340032 | tf_op jit(solution)/shard_map/pallas_call | solution.py:109
  32.8 2.2 %shard_map.51 = (bf16[128,1792]{1,0:T(8,128)(2,1)S(1)}, bf16[128,1792]{1,0:T(8,128)(2,1)S(1)}) custom-call(bf16[64,2048]{1,0:T(8,128)(2,1)S(1)} %copy-done, bf16[64,2048]{1,0:T(8,128)(2,1)S(1)} %collective-permute-done.refs_1_.refs_5_, bf16[64,2048]{1,0:T(8,128)(2,1)S(1)} %collective-permute-done.1.refs_2_.refs_6_, ...), custom_call_target="tpu_custom_call" | custom-call | flops 1879048192 | bytes 7340032 | tf_op jit(solution)/shard_map/pallas_call | solution.py:109
  35.0 0.6 collective-permute-start.17
  35.7 0.4 collective-permute-start.18
  36.1 0.5 collective-permute-done.8.refs_1_.refs_9_
  36.6 2.2 %shard_map.58 = (bf16[128,1792]{1,0:T(8,128)(2,1)S(1)}, bf16[128,1792]{1,0:T(8,128)(2,1)S(1)}) custom-call(bf16[64,2048]{1,0:T(8,128)(2,1)S(1)} %collective-permute-done.7.refs_0_.refs_8_, bf16[64,2048]{1,0:T(8,128)(2,1)S(1)} %collective-permute-done.8.refs_1_.refs_9_, bf16[64,2048]{1,0:T(8,128)(2,1)S(1)} %collective-permute-done.9.refs_2_.refs_10_, ...), custom_call_target="tpu_custom_call" | custom-call | flops 1879048192 | bytes 7340032 | tf_op jit(solution)/shard_map/pallas_call | solution.py:109
  38.9 2.2 %shard_map.56 = (bf16[128,1792]{1,0:T(8,128)(2,1)S(1)}, bf16[128,1792]{1,0:T(8,128)(2,1)S(1)}) custom-call(bf16[64,2048]{1,0:T(8,128)(2,1)S(1)} %collective-permute-done.7.refs_0_.refs_8_, bf16[64,2048]{1,0:T(8,128)(2,1)S(1)} %collective-permute-done.8.refs_1_.refs_9_, bf16[64,2048]{1,0:T(8,128)(2,1)S(1)} %collective-permute-done.9.refs_2_.refs_10_, ...), custom_call_target="tpu_custom_call" | custom-call | flops 1879048192 | bytes 7340032 | tf_op jit(solution)/shard_map/pallas_call | solution.py:109
  41.1 0.6 collective-permute-start.11
  41.7 0.1 shard_map.55
  41.8 0.6 collective-permute-start.6
  42.5 1.6 %collective-permute-start.5 = (bf16[64,1792]{1,0:T(8,128)(2,1)S(1)}, bf16[64,1792]{1,0:T(8,128)(2,1)S(1)}, u32[]{:S(2)}, u32[]{:S(2)}) collective-permute-start(bf16[64,1792]{1,0:T(8,128)(2,1)S(1)} %get-tuple-element.28), channel_id=1, source_target_pairs={{0,8},{8,0},{1,9},{9,1},{2,10},{10,2},{3,11},{11,3},{4,12},{12,4},... | collective-permute-start | bytes 688136 | tf_op jit(solution)/shard_map/ppermute | solution.py:267
  44.2 0.6 collective-permute-start.14
  44.8 0.1 shard_map.57
  44.9 5.4 %collective-permute-done.6.refs_3_ = bf16[64,1792]{1,0:T(8,128)(2,1)S(1)} collective-permute-done((bf16[64,1792]{1,0:T(8,128)(2,1)S(1)}, bf16[64,1792]{1,0:T(8,128)(2,1)S(1)}, u32[]{:S(2)}, u32[]{:S(2)}) %collective-permute-start.6) | collective-permute-done | bytes 229408 | tf_op jit(solution)/shard_map/ppermute | solution.py:267
  50.3 0.5 collective-permute-start.13
  50.9 4.4 %collective-permute-done.5.refs_2_ = bf16[64,1792]{1,0:T(8,128)(2,1)S(1)} collective-permute-done((bf16[64,1792]{1,0:T(8,128)(2,1)S(1)}, bf16[64,1792]{1,0:T(8,128)(2,1)S(1)}, u32[]{:S(2)}, u32[]{:S(2)}) %collective-permute-start.5) | collective-permute-done | bytes 229408 | tf_op jit(solution)/shard_map/ppermute | solution.py:267
  55.2 4.9 %collective-permute-done.14.refs_7_ = bf16[64,1792]{1,0:T(8,128)(2,1)S(1)} collective-permute-done((bf16[64,1792]{1,0:T(8,128)(2,1)S(1)}, bf16[64,1792]{1,0:T(8,128)(2,1)S(1)}, u32[]{:S(2)}, u32[]{:S(2)}) %collective-permute-start.14) | collective-permute-done | bytes 229408 | tf_op jit(solution)/shard_map/ppermute | solution.py:267
  60.2 4.0 %collective-permute-done.13.refs_6_ = bf16[64,1792]{1,0:T(8,128)(2,1)S(1)} collective-permute-done((bf16[64,1792]{1,0:T(8,128)(2,1)S(1)}, bf16[64,1792]{1,0:T(8,128)(2,1)S(1)}, u32[]{:S(2)}, u32[]{:S(2)}) %collective-permute-start.13) | collective-permute-done | bytes 229408 | tf_op jit(solution)/shard_map/ppermute | solution.py:267
  64.1 0.4 shard_map.60
  64.6 10.1 %shard_map.62 = (f32[3584,2048]{1,0:T(8,128)}, bf16[512,2048]{1,0:T(8,128)(2,1)S(1)}) custom-call(bf16[128,3584]{1,0:T(8,128)(2,1)S(1)} %copy-done.1, bf16[128,3584]{1,0:T(8,128)(2,1)S(1)} %collective-permute-done.16.refs_1_, bf16[128,3584]{1,0:T(8,128)(2,1)S(1)} %collective-permute-done.17.refs_2_, bf16[128,3584]{1,0:T(8,128)(2,1)S(1)} %collective-permute-done.18.refs_3_, ...), custom_call_target="tpu_custom_call" | custom-call | flops 6979321856 | bytes 27262976 | tf_op jit(solution)/shard_map/pallas_call | solution.py:174
  74.8 2.1 %shard_map.63 = f32[3584,2048]{1,0:T(8,128)} custom-call(bf16[128,3584]{1,0:T(8,128)(2,1)S(1)} %copy-done.1, bf16[128,3584]{1,0:T(8,128)(2,1)S(1)} %collective-permute-done.16.refs_1_, bf16[128,3584]{1,0:T(8,128)(2,1)S(1)} %collective-permute-done.17.refs_2_, bf16[128,3584]{1,0:T(8,128)(2,1)S(1)} %collective-permute-done.18.refs_3_, ...), custom_call_target="tpu_custom_call", output_to_operand_aliasing={{}: (5, {})} | custom-call | flops 536870912 | bytes 2097152 | tf_op jit(solution)/shard_map/pallas_call | solution.py:174
  76.8 1.0 %shard_map.61 = bf16[128,3584]{1,0:T(8,128)(2,1)} custom-call(bf16[64,3584]{1,0:T(8,128)(2,1)S(1)} %get-tuple-element.38.kept, bf16[64,3584]{1,0:T(8,128)(2,1)S(1)} %collective-permute-done.15.got), custom_call_target="tpu_custom_call" | custom-call | flops 458752 | bytes 1835008 | tf_op jit(solution)/shard_map/pallas_call | solution.py:187
  (24 shorter events, 0.6 us)
Async XLA Ops:
  0.6 35.1 %collective-permute-start.16 = (bf16[128,3584]{1,0:T(8,128)(2,1)}, bf16[128,3584]{1,0:T(8,128)(2,1)S(1)}, u32[]{:S(2)}, u32[]{:S(2)}) collective-permute-start(bf16[128,3584]{1,0:T(8,128)(2,1)} %refs_0_.7), channel_id=1, source_target_pairs={{0,8},{8,0},{1,9},{9,1},{2,10},{10,2},{3,11},{11,3},{4,12},{12,4},... | collective-permute-start | bytes 2752520 | tf_op jit(solution)/shard_map/ppermute | solution.py:267
  3.7 11.2 %collective-permute-start.1 = (bf16[64,2048]{1,0:T(8,128)(2,1)}, bf16[64,2048]{1,0:T(8,128)(2,1)S(1)}, u32[]{:S(2)}, u32[]{:S(2)}) collective-permute-start(bf16[64,2048]{1,0:T(8,128)(2,1)} %refs_4_.1), channel_id=1, source_target_pairs={{0,2},{1,3},{2,4},{3,5},{4,6},{5,7},{6,0},{7,1},{8,10},{9,11},{10,... | collective-permute-start | bytes 786440 | tf_op jit(solution)/shard_map/ppermute | solution.py:267
  5.2 18.2 %collective-permute-start.9 = (bf16[64,2048]{1,0:T(8,128)(2,1)}, bf16[64,2048]{1,0:T(8,128)(2,1)S(1)}, u32[]{:S(2)}, u32[]{:S(2)}) collective-permute-start(bf16[64,2048]{1,0:T(8,128)(2,1)} %refs_4_.1), channel_id=1, source_target_pairs={{0,6},{1,7},{2,0},{3,1},{4,2},{5,3},{6,4},{7,5},{8,14},{9,15},{10,... | collective-permute-start | bytes 786440 | tf_op jit(solution)/shard_map/ppermute | solution.py:267
  14.9 10.2 %collective-permute-start.2 = (bf16[64,2048]{1,0:T(8,128)(2,1)S(1)}, bf16[64,2048]{1,0:T(8,128)(2,1)S(1)}, u32[]{:S(2)}, u32[]{:S(2)}) collective-permute-start(bf16[64,2048]{1,0:T(8,128)(2,1)S(1)} %collective-permute-done.1.refs_2_.refs_6_), channel_id=1, source_target_pairs={{0,1},{1,0},{2,3},{3,2},{4,5},{5,4},{6,7},{7,6},{8,9},{9,8},{10,11... | collective-permute-start | bytes 786440 | tf_op jit(solution)/shard_map/ppermute | solution.py:267
  16.4 14.1 %collective-permute-start = (bf16[64,2048]{1,0:T(8,128)(2,1)}, bf16[64,2048]{1,0:T(8,128)(2,1)S(1)}, u32[]{:S(2)}, u32[]{:S(2)}) collective-permute-start(bf16[64,2048]{1,0:T(8,128)(2,1)} %refs_4_.1), channel_id=1, source_target_pairs={{0,1},{1,0},{2,3},{3,2},{4,5},{5,4},{6,7},{7,6},{8,9},{9,8},{10,11... | collective-permute-start | bytes 786440 | tf_op jit(solution)/shard_map/ppermute | solution.py:267
  20.1 10.4 %copy-start = (bf16[64,2048]{1,0:T(8,128)(2,1)S(1)}, bf16[64,2048]{1,0:T(8,128)(2,1)}, u32[]{:S(2)}) copy-start(bf16[64,2048]{1,0:T(8,128)(2,1)} %refs_4_.1) | copy-start | bytes 786436
  20.1 14.9 %copy-start.1 = (bf16[128,3584]{1,0:T(8,128)(2,1)S(1)}, bf16[128,3584]{1,0:T(8,128)(2,1)}, u32[]{:S(2)}) copy-start(bf16[128,3584]{1,0:T(8,128)(2,1)} %refs_0_.7) | copy-start | bytes 2752516
  23.4 11.6 %collective-permute-start.7 = (bf16[64,2048]{1,0:T(8,128)(2,1)S(1)}, bf16[64,2048]{1,0:T(8,128)(2,1)S(1)}, u32[]{:S(2)}, u32[]{:S(2)}) collective-permute-start(bf16[64,2048]{1,0:T(8,128)(2,1)S(1)} %collective-permute-done.1.refs_2_.refs_6_), channel_id=1, source_target_pairs={{0,2},{1,3},{2,4},{3,5},{4,6},{5,7},{6,0},{7,1},{8,10},{9,11},{10,... | collective-permute-start | bytes 786440 | tf_op jit(solution)/shard_map/ppermute | solution.py:267
  23.5 12.1 %collective-permute-start.10 = (bf16[64,2048]{1,0:T(8,128)(2,1)S(1)}, bf16[64,2048]{1,0:T(8,128)(2,1)S(1)}, u32[]{:S(2)}, u32[]{:S(2)}) collective-permute-start(bf16[64,2048]{1,0:T(8,128)(2,1)S(1)} %collective-permute-done.9.refs_2_.refs_10_), channel_id=1, source_target_pairs={{0,1},{1,0},{2,3},{3,2},{4,5},{5,4},{6,7},{7,6},{8,9},{9,8},{10,11... | collective-permute-start | bytes 786440 | tf_op jit(solution)/shard_map/ppermute | solution.py:267
  25.1 11.5 %collective-permute-start.8 = (bf16[64,2048]{1,0:T(8,128)(2,1)S(1)}, bf16[64,2048]{1,0:T(8,128)(2,1)S(1)}, u32[]{:S(2)}, u32[]{:S(2)}) collective-permute-start(bf16[64,2048]{1,0:T(8,128)(2,1)S(1)} %collective-permute-done.2.refs_3_.refs_7_), channel_id=1, source_target_pairs={{0,2},{1,3},{2,4},{3,5},{4,6},{5,7},{6,0},{7,1},{8,10},{9,11},{10,... | collective-permute-start | bytes 786440 | tf_op jit(solution)/shard_map/ppermute | solution.py:267
  32.7 8.4 %collective-permute-start.4 = (bf16[128,1792]{1,0:T(8,128)(2,1)S(1)}, bf16[128,1792]{1,0:T(8,128)(2,1)S(1)}, u32[]{:S(2)}, u32[]{:S(2)}) collective-permute-start(bf16[128,1792]{1,0:T(8,128)(2,1)S(1)} %get-tuple-element.26), channel_id=1, source_target_pairs={{0,16},{16,0},{1,17},{17,1},{2,18},{18,2},{3,19},{19,3},{4,20},{20... | collective-permute-start | bytes 1376264 | tf_op jit(solution)/shard_map/ppermute | solution.py:267
  35.0 29.6 %collective-permute-start.17 = (bf16[128,3584]{1,0:T(8,128)(2,1)S(1)}, bf16[128,3584]{1,0:T(8,128)(2,1)S(1)}, u32[]{:S(2)}, u32[]{:S(2)}) collective-permute-start(bf16[128,3584]{1,0:T(8,128)(2,1)S(1)} %copy-done.1), channel_id=1, source_target_pairs={{0,16},{16,0},{1,17},{17,1},{2,18},{18,2},{3,19},{19,3},{4,20},{20... | collective-permute-start | bytes 2752520 | tf_op jit(solution)/shard_map/ppermute | solution.py:267
  35.6 6.2 %collective-permute-start.3 = (bf16[128,1792]{1,0:T(8,128)(2,1)S(1)}, bf16[128,1792]{1,0:T(8,128)(2,1)S(1)}, u32[]{:S(2)}, u32[]{:S(2)}) collective-permute-start(bf16[128,1792]{1,0:T(8,128)(2,1)S(1)} %get-tuple-element.23), channel_id=1, source_target_pairs={{0,16},{16,0},{1,17},{17,1},{2,18},{18,2},{3,19},{19,3},{4,20},{20... | collective-permute-start | bytes 1376264 | tf_op jit(solution)/shard_map/ppermute | solution.py:267
  35.7 28.9 %collective-permute-start.18 = (bf16[128,3584]{1,0:T(8,128)(2,1)S(1)}, bf16[128,3584]{1,0:T(8,128)(2,1)S(1)}, u32[]{:S(2)}, u32[]{:S(2)}) collective-permute-start(bf16[128,3584]{1,0:T(8,128)(2,1)S(1)} %collective-permute-done.16.refs_1_), channel_id=1, source_target_pairs={{0,16},{16,0},{1,17},{17,1},{2,18},{18,2},{3,19},{19,3},{4,20},{20... | collective-permute-start | bytes 2752520 | tf_op jit(solution)/shard_map/ppermute | solution.py:267
  38.8 3.7 %collective-permute-start.12 = (bf16[128,1792]{1,0:T(8,128)(2,1)S(1)}, bf16[128,1792]{1,0:T(8,128)(2,1)S(1)}, u32[]{:S(2)}, u32[]{:S(2)}) collective-permute-start(bf16[128,1792]{1,0:T(8,128)(2,1)S(1)} %get-tuple-element.34), channel_id=1, source_target_pairs={{0,16},{16,0},{1,17},{17,1},{2,18},{18,2},{3,19},{19,3},{4,20},{20... | collective-permute-start | bytes 1376264 | tf_op jit(solution)/shard_map/ppermute | solution.py:267
  41.1 3.1 %collective-permute-start.11 = (bf16[128,1792]{1,0:T(8,128)(2,1)S(1)}, bf16[128,1792]{1,0:T(8,128)(2,1)S(1)}, u32[]{:S(2)}, u32[]{:S(2)}) collective-permute-start(bf16[128,1792]{1,0:T(8,128)(2,1)S(1)} %get-tuple-element.31), channel_id=1, source_target_pairs={{0,16},{16,0},{1,17},{17,1},{2,18},{18,2},{3,19},{19,3},{4,20},{20... | collective-permute-start | bytes 1376264 | tf_op jit(solution)/shard_map/ppermute | solution.py:267
  41.8 8.5 %collective-permute-start.6 = (bf16[64,1792]{1,0:T(8,128)(2,1)S(1)}, bf16[64,1792]{1,0:T(8,128)(2,1)S(1)}, u32[]{:S(2)}, u32[]{:S(2)}) collective-permute-start(bf16[64,1792]{1,0:T(8,128)(2,1)S(1)} %get-tuple-element.29), channel_id=1, source_target_pairs={{0,8},{8,0},{1,9},{9,1},{2,10},{10,2},{3,11},{11,3},{4,12},{12,4},... | collective-permute-start | bytes 688136 | tf_op jit(solution)/shard_map/ppermute | solution.py:267
  42.5 12.7 %collective-permute-start.5 = (bf16[64,1792]{1,0:T(8,128)(2,1)S(1)}, bf16[64,1792]{1,0:T(8,128)(2,1)S(1)}, u32[]{:S(2)}, u32[]{:S(2)}) collective-permute-start(bf16[64,1792]{1,0:T(8,128)(2,1)S(1)} %get-tuple-element.28), channel_id=1, source_target_pairs={{0,8},{8,0},{1,9},{9,1},{2,10},{10,2},{3,11},{11,3},{4,12},{12,4},... | collective-permute-start | bytes 688136 | tf_op jit(solution)/shard_map/ppermute | solution.py:267
  44.2 16.0 %collective-permute-start.14 = (bf16[64,1792]{1,0:T(8,128)(2,1)S(1)}, bf16[64,1792]{1,0:T(8,128)(2,1)S(1)}, u32[]{:S(2)}, u32[]{:S(2)}) collective-permute-start(bf16[64,1792]{1,0:T(8,128)(2,1)S(1)} %get-tuple-element.37), channel_id=1, source_target_pairs={{0,8},{8,0},{1,9},{9,1},{2,10},{10,2},{3,11},{11,3},{4,12},{12,4},... | collective-permute-start | bytes 688136 | tf_op jit(solution)/shard_map/ppermute | solution.py:267
  50.3 13.8 %collective-permute-start.13 = (bf16[64,1792]{1,0:T(8,128)(2,1)S(1)}, bf16[64,1792]{1,0:T(8,128)(2,1)S(1)}, u32[]{:S(2)}, u32[]{:S(2)}) collective-permute-start(bf16[64,1792]{1,0:T(8,128)(2,1)S(1)} %get-tuple-element.36), channel_id=1, source_target_pairs={{0,8},{8,0},{1,9},{9,1},{2,10},{10,2},{3,11},{11,3},{4,12},{12,4},... | collective-permute-start | bytes 688136 | tf_op jit(solution)/shard_map/ppermute | solution.py:267
  64.5 12.3 %collective-permute-start.15 = (bf16[64,3584]{1,0:T(8,128)(2,1)S(1)}, bf16[64,3584]{1,0:T(8,128)(2,1)S(1)}, u32[]{:S(2)}, u32[]{:S(2)}) collective-permute-start(bf16[64,3584]{1,0:T(8,128)(2,1)S(1)} %get-tuple-element.39), channel_id=1, source_target_pairs={{0,16},{16,0},{1,17},{17,1},{2,18},{18,2},{3,19},{19,3},{4,20},{20... | collective-permute-start | bytes 1376264 | tf_op jit(solution)/shard_map/ppermute | solution.py:267
